TPU v7x, 128 devices: a whole 4x4x4 slice. The times are simulated.
128 devices in a mesh: frame: 8 (over x, core), seq: 16 (over y, z).
Axes of the slice: x: 4, y: 4, z: 4, core: 2. Of those that a mesh axis runs over, the one named last changes fastest.
Arguments:
- vit_states: bfloat16 [256, 256, 1280], P(('frame', 'seq')), may hold values from -6 to 6
- frame_slot: int32 [128], replicated, may hold values from 0 to 255, as said below
- patch_count: int32 [128], replicated, may hold values from 208 to 256, as said below
- vis_start: int32 [128], replicated, may hold values from 0 to 16383, as said below
- text_embed: bfloat16 [128, 128, 4096], P(None, ('frame', 'seq')), may hold values from -6 to 6
- vit_ln_gain: float32 [1280], replicated, may hold values from 0.25 to 1.75
- vit_ln_bias: float32 [1280], replicated, may hold values from -1.5 to 1.5
- vit_qkv_w: bfloat16 [1280, 3840], P('seq'), may hold values from -0.15625 to 0.15625
- vit_qkv_b: float32 [3840], replicated, may hold values from -1.5 to 1.5
- vit_out_w: bfloat16 [1280, 1280], P('seq'), may hold values from -0.15625 to 0.15625
- vit_out_b: float32 [1280], replicated, may hold values from -1.5 to 1.5
- proj_w: bfloat16 [1280, 4096], replicated, may hold values from -0.15625 to 0.15625
- proj_b: float32 [4096], replicated, may hold values from -1.5 to 1.5
- attn_gain: float32 [4096], replicated, may hold values from 0.25 to 1.75
- wq: bfloat16 [4096, 2048], P(None, 'frame'), may hold values from -0.09375 to 0.09375
- wk: bfloat16 [4096, 1024], P(None, 'frame'), may hold values from -0.09375 to 0.09375
- wv: bfloat16 [4096, 1024], P(None, 'frame'), may hold values from -0.09375 to 0.09375
- wo: bfloat16 [2048, 4096], P('frame'), may hold values from -0.125 to 0.125
Outputs:
- mixed: bfloat16 [128, 128, 4096], P(None, ('frame', 'seq'))
Inputs may be any that keep to these rules, and one draw needn't show every extreme that they name: Frame t sits in slot frame_slot[t]; slot k of the device with index d (axes frame then seq) is d * 2 + k; no slot holds two frames. The two devices with frame indices 2i and 2i+1 and the same seq index hold exactly two frames between them; some device holds 2 frames. `patch_count`: A multiple of 4; some frame has 256 patches. Frame t's patch_count[t] / 4 visual positions start at vis_start[t] and lie within positions t * 128 to (t + 1) * 128 - 1.
All inputs are finite; a program needn't handle non-finite values.
Results may differ from a plain program's by a relative error of at most 0.015.
Values may be sent and summed in bfloat16 or wider, within the bound.
No kernel may reach another device: no remote copies, remote signals or barrier semaphores. Data moves between devices by JAX's collectives and lax.ppermute only.
A program may use at most 128 MiB of HBM per device.

v0:
```python
import math

import jax
import jax.numpy as jnp
from jax import lax
from jax.sharding import PartitionSpec as P

VHEADS = 16
HEAD_WIDTH = 128


rope_theta = 500000.0
vit_epsilon = 1e-06
norm_epsilon = 1e-05
masked_score = -1e30


def partner_2(value, axis, stride):
    mask = 2**stride
    pairs = [(source, source ^ mask) for source in range(lax.axis_size(axis))]
    return lax.ppermute(value, axis, pairs)


def in_one_piece(arrays, axis, dim, along):
    widths = [a.shape[along] for a in arrays]
    both = jnp.concatenate(arrays, axis=along)
    result = lax.all_gather(both, axis, axis=dim, tiled=True)
    return tuple(jnp.split(result, [sum(widths[:k]) for k in range(1, len(widths))], axis=along))


def apply_rotary(values, rotary_angles):
    half_width = values.shape[-1] // 2
    first_half = values[..., :half_width]
    second_half = values[..., half_width:]
    cosine = jnp.cos(rotary_angles)
    sine_part = jnp.sin(rotary_angles)
    return jnp.concatenate(
        [
            first_half * cosine - second_half * sine_part,
            second_half * cosine + first_half * sine_part,
        ],
        axis=-1,
    )


def rope_angles(positions, head_size):
    exponents = jnp.arange(0, head_size, 2).astype(jnp.float32) / head_size
    inverse = jnp.power(jnp.float32(rope_theta), -exponents)
    return positions.astype(jnp.float32)[:, None] * inverse[None, :]


def add_columns(left, shard_piece):
    return jnp.dot(left, shard_piece, preferred_element_type=jnp.float32)


def per_device(
    vit_states,
    frame_slot,
    patch_count,
    vis_start,
    text_embed,
    vit_ln_gain,
    vit_ln_bias,
    vit_qkv_w,
    vit_qkv_b,
    vit_out_w,
    vit_out_b,
    proj_w,
    proj_b,
    attn_gain,
    wq,
    wk,
    wv,
    wo,
):
    frames_n = lax.axis_size("frame")
    seqs_n = lax.axis_size("seq")
    devices_n = frames_n * seqs_n
    my_frame = lax.axis_index("frame")
    my_seq = lax.axis_index("seq")
    my_device = my_frame * seqs_n + my_seq
    slots_held = vit_states.shape[0]
    frame_max = vit_states.shape[1]
    width_vit = vit_states.shape[2]
    vis_max = frame_max // 4
    own_rows = text_embed.shape[0]
    laps = (vis_max + devices_n - 1) // devices_n
    frame_ids = jnp.arange(frame_slot.shape[0])
    holder = frame_slot // slots_held
    holder_frame = holder // seqs_n
    pair_low = (holder_frame - holder_frame % 2) * seqs_n + holder % seqs_n
    pair_order = holder_frame % 2 * slots_held + frame_slot % slots_held
    same_pair = pair_low[:, None] == pair_low[None, :]
    earlier = pair_order[None, :] < pair_order[:, None]
    pair_rank = jnp.sum((same_pair & earlier).astype(jnp.int32), axis=1)
    partner = partner_2(vit_states, "frame", 0)
    low_side = my_frame % 2 == 0
    four_slots = jnp.where(
        low_side,
        jnp.concatenate([vit_states, partner], 0),
        jnp.concatenate([partner, vit_states], 0),
    )
    my_low = (my_frame - my_frame % 2) * seqs_n + my_seq
    picked = (pair_low == my_low) & (pair_rank == my_frame % 2)
    my_frame_id = jnp.sum(jnp.where(picked, frame_ids, 0))
    my_order = jnp.sum(jnp.where(picked, pair_order, 0))
    states = lax.dynamic_slice_in_dim(four_slots, my_order, 1, 0)
    slots_n = 1
    slot_frames = jnp.reshape(my_frame_id, (1,))
    slot_live = jnp.ones((1,), jnp.bool_)
    source_device = pair_low + pair_rank * seqs_n
    slot_count = jnp.where(slot_live, patch_count[slot_frames], frame_max)
    slot_start = vis_start[slot_frames]
    patch_rows = states.reshape(slots_n * frame_max, width_vit)
    rows_wide = patch_rows.astype(jnp.float32)
    average = jnp.mean(rows_wide, axis=1, keepdims=True)
    centred = rows_wide - average
    spread = jnp.mean(centred * centred, axis=1, keepdims=True)
    normed_states = (centred * lax.rsqrt(spread + vit_epsilon) * vit_ln_gain + vit_ln_bias).astype(
        jnp.bfloat16
    )
    projected_vit = add_columns(normed_states, lax.all_gather(vit_qkv_w, "seq", axis=0, tiled=True))
    projected_vit = (projected_vit + vit_qkv_b).astype(jnp.bfloat16)
    head_size = width_vit // VHEADS
    shaped = projected_vit.reshape(slots_n, frame_max, 3, VHEADS, head_size)
    scores = jnp.einsum(
        "sqhd,skhd->shqk", shaped[:, :, 0], shaped[:, :, 1], preferred_element_type=jnp.float32
    ) / math.sqrt(head_size)
    key_live = jnp.arange(frame_max)[None, :] < slot_count[:, None]
    scores = jnp.where(key_live[:, None, None, :], scores, masked_score)
    highest = jnp.max(scores, axis=-1, keepdims=True)
    weights = jnp.exp(scores - highest)
    probabilities = (weights / jnp.sum(weights, axis=-1, keepdims=True)).astype(jnp.bfloat16)
    context_vit = jnp.einsum(
        "shqk,skhd->sqhd", probabilities, shaped[:, :, 2], preferred_element_type=jnp.float32
    ).astype(jnp.bfloat16)
    context_vit = context_vit.reshape(patch_rows.shape[0], width_vit)
    attended = add_columns(context_vit, lax.all_gather(vit_out_w, "seq", axis=0, tiled=True))
    hidden = (rows_wide + attended + vit_out_b).astype(jnp.bfloat16)
    pooled = jnp.mean(
        hidden.astype(jnp.float32).reshape(slots_n, vis_max, 4, width_vit), axis=2
    ).astype(jnp.bfloat16)
    owners = jnp.arange(devices_n)
    lap_ids = jnp.arange(laps)
    distance = jnp.mod(owners[:, None] - slot_start[None, :], devices_n)
    token_ids = distance[:, :, None] + lap_ids[None, None, :] * devices_n
    sent_live = (token_ids < (slot_count // 4)[None, :, None]) & slot_live[None, :, None]
    token_clip = jnp.minimum(token_ids, vis_max - 1)
    slot_ids = jnp.arange(slots_n)[None, :, None]
    outgoing = jnp.where(
        sent_live[..., None], pooled[slot_ids, token_clip], jnp.zeros((), jnp.bfloat16)
    )
    arrived = lax.all_to_all(outgoing, ("frame", "seq"), split_axis=0, concat_axis=0, tiled=True)
    local_ids = jnp.arange(own_rows)
    positions = local_ids * devices_n + my_device
    token_frame = positions // own_rows
    within = positions - vis_start[token_frame]
    is_visual = (within >= 0) & (within < patch_count[token_frame] // 4)
    within_clip = jnp.clip(within, 0, vis_max - 1)
    flat_index = source_device[token_frame] * slots_n * laps + within_clip // devices_n
    table = arrived.reshape(devices_n * slots_n * laps, arrived.shape[-1])
    fetched = table[flat_index]
    fetched = (jnp.dot(fetched, proj_w, preferred_element_type=jnp.float32) + proj_b).astype(
        jnp.bfloat16
    )
    text_rows = text_embed.reshape(own_rows, text_embed.shape[-1])
    merged = jnp.where(is_visual[:, None], fetched, text_rows)
    merged_wide = merged.astype(jnp.float32)
    normed_tok = (
        merged_wide
        * lax.rsqrt(jnp.mean(merged_wide * merged_wide, axis=1, keepdims=True) + norm_epsilon)
        * attn_gain
    ).astype(jnp.bfloat16)
    shard_piece = lax.all_gather(normed_tok, "frame", axis=0, tiled=True)
    projected = jnp.concatenate(
        [
            jnp.dot(shard_piece, wq, preferred_element_type=jnp.float32),
            jnp.dot(shard_piece, wk, preferred_element_type=jnp.float32),
            jnp.dot(shard_piece, wv, preferred_element_type=jnp.float32),
        ],
        axis=1,
    )
    query_width = wq.shape[1]
    kv_width = wk.shape[1]
    group_rows = projected.shape[0]
    kv_heads = kv_width // HEAD_WIDTH
    query_heads = query_width // HEAD_WIDTH
    row_ids = jnp.arange(group_rows)
    group_positions = row_ids % own_rows * devices_n + row_ids // own_rows * seqs_n + my_seq
    rotary_angles = rope_angles(group_positions, HEAD_WIDTH)[:, None, :]
    query_matrix = apply_rotary(
        projected[:, :query_width].reshape(group_rows, query_heads, HEAD_WIDTH), rotary_angles
    ).astype(jnp.bfloat16)
    keys_own = apply_rotary(
        projected[:, query_width : query_width + kv_width].reshape(
            group_rows, kv_heads, HEAD_WIDTH
        ),
        rotary_angles,
    ).astype(jnp.bfloat16)
    values_own = (
        projected[:, query_width + kv_width :]
        .astype(jnp.bfloat16)
        .reshape(group_rows, kv_heads, HEAD_WIDTH)
    )
    grouped_rows = query_matrix.reshape(group_rows, kv_heads, query_heads // kv_heads, HEAD_WIDTH)
    group_size = query_heads // kv_heads
    start_state = (
        jnp.full((kv_heads, group_size, group_rows), masked_score, jnp.float32),
        jnp.zeros((kv_heads, group_size, group_rows), jnp.float32),
        jnp.zeros((kv_heads, group_size, group_rows, HEAD_WIDTH), jnp.float32),
    )
    carry = start_state
    key_piece, value_piece = in_one_piece((keys_own, values_own), "seq", 0, 1)
    piece_rows = key_piece.shape[0]
    inner_rows = math.gcd(piece_rows, 1024)
    steps_n = piece_rows // inner_rows
    key_blocks = key_piece.reshape(steps_n, inner_rows, kv_heads, HEAD_WIDTH)
    value_blocks = value_piece.reshape(steps_n, inner_rows, kv_heads, HEAD_WIDTH)
    block_offsets = inner_rows * jnp.arange(steps_n)

    def visit(running, operands):
        running_max, denominator, weighted = running
        key_block, value_block, block_offset = operands
        gathered_ids = block_offset + jnp.arange(inner_rows)
        seq_of = gathered_ids // group_rows
        inner_ids = gathered_ids % group_rows
        key_positions = inner_ids % own_rows * devices_n + inner_ids // own_rows * seqs_n + seq_of
        block_scores = jnp.einsum(
            "qkgd,nkd->kgqn", grouped_rows, key_block, preferred_element_type=jnp.float32
        ) / math.sqrt(HEAD_WIDTH)
        allowed = key_positions[None, :] <= group_positions[:, None]
        block_scores = jnp.where(allowed[None, None], block_scores, masked_score)
        new_max = jnp.maximum(running_max, jnp.max(block_scores, axis=-1))
        expd = jnp.where(allowed[None, None], jnp.exp(block_scores - new_max[..., None]), 0.0)
        rescale = jnp.exp(running_max - new_max)
        denominator = denominator * rescale + jnp.sum(expd, axis=-1)
        weighted = weighted * rescale[..., None] + jnp.einsum(
            "kgqn,nkd->kgqd",
            expd.astype(jnp.bfloat16),
            value_block,
            preferred_element_type=jnp.float32,
        )
        return ((new_max, denominator, weighted), None)

    carry, unused = lax.scan(visit, carry, (key_blocks, value_blocks, block_offsets))
    final_max, denominator, weighted = carry
    context_tok = (weighted / denominator[..., None]).astype(jnp.bfloat16)
    context_tok = jnp.transpose(context_tok, (2, 0, 1, 3)).reshape(group_rows, query_width)
    summed = lax.psum_scatter(
        jnp.dot(context_tok, wo, preferred_element_type=jnp.float32).astype(jnp.bfloat16),
        "frame",
        scatter_dimension=0,
        tiled=True,
    )
    return summed.reshape(own_rows, 1, wo.shape[1])


def solution(mesh):
    return jax.shard_map(
        per_device,
        mesh=mesh,
        in_specs=(
            P(("frame", "seq"), None, None),
            P(),
            P(),
            P(),
            P(None, ("frame", "seq"), None),
            P(),
            P(),
            P("seq", None),
            P(),
            P("seq", None),
            P(),
            P(),
            P(),
            P(),
            P(None, "frame"),
            P(None, "frame"),
            P(None, "frame"),
            P("frame", None),
        ),
        out_specs=P(None, ("frame", "seq"), None),
        check_vma=False,
    )
```

profile of v0, /device:TPU:1, one launch (start us, length us, event | category | flops | bytes accessed | tf_op | source)
XLA Modules:
  0.0 679.3 jit_solution(15090803585346122329)
XLA Ops:
  29.6 60.5 %all-gather.5.cloned.1.call-done = bf16[1280,3840]{1,0:T(8,128)(2,1)} async-done(((bf16[80,3840]{1,0:T(8,128)(2,1)}), bf16[1280,3840]{1,0:T(8,128)(2,1)}) %all-gather.5.cloned.1.call-update) | async-done | bytes 9830416 | tf_op jit(solution)/shard_map/all_gather | solution.py:122
  90.1 7.9 %fusion.52 = bf16[256,3840]{1,0:T(8,128)(2,1)} fusion(bf16[1280,3840]{1,0:T(8,128)(2,1)} %all-gather.5.cloned.1.call-done, f32[3840]{0:T(1024)S(1)} %copy-done.7, bf16[1,256,1280]{2,1,0:T(8,128)(2,1)S(1)} %get-tuple-element.286, f32[1280]{0:T(1024)S(1)} %copy-done.8, f32[1280]{0:T(1024)S(1)} %copy-done.9, f32[256]{0:T(256)S(1)} %add_rsqrt_fusion, ...), kind=kOutput, calls=%fused_computation.79 | convolution fusion | flops 2520514560 | bytes 12479488 | tf_op jit(solution)/shard_map/dot_general | solution.py:53
  98.0 4.0 copy.59
  105.7 2.4 fusion.67
  108.2 31.7 %all-gather.7.cloned.1.call-done = bf16[1280,1280]{1,0:T(8,128)(2,1)} async-done(((bf16[80,1280]{1,0:T(8,128)(2,1)}), bf16[1280,1280]{1,0:T(8,128)(2,1)}) %all-gather.7.cloned.1.call-update) | async-done | bytes 3276816 | tf_op jit(solution)/shard_map/all_gather | solution.py:138
  139.9 4.2 fusion.59
  144.1 2.6 reshape.802
  152.9 7.4 %all-to-all-start = ((bf16[128,2,640]{2,1,0:T(2,128)(2,1)}), bf16[128,2,640]{2,1,0:T(2,128)(2,1)S(1)}, u32[]{:S(2)}, u32[]{:S(2)}) async-start(bf16[128,2,640]{2,1,0:T(2,128)(2,1)} %reshape.851), calls=%async_computation | async-start | bytes 655360 | tf_op jit(solution)/shard_map/all_to_all | solution.py:153
  160.6 11.6 %all-to-all-done = bf16[128,2,640]{2,1,0:T(2,128)(2,1)S(1)} async-done(((bf16[128,2,640]{2,1,0:T(2,128)(2,1)}), bf16[128,2,640]{2,1,0:T(2,128)(2,1)S(1)}, u32[]{:S(2)}, u32[]{:S(2)}) %all-to-all-start) | async-done | bytes 327712 | tf_op jit(solution)/shard_map/all_to_all | solution.py:153
  173.5 6.3 multiply_reduce_fusion
  181.1 46.0 %all-gather.9.cloned.1.call-done = bf16[1024,4096]{1,0:T(8,128)(2,1)} async-done(((bf16[128,4096]{1,0:T(8,128)(2,1)}), bf16[1024,4096]{1,0:T(8,128)(2,1)}) %all-gather.9.cloned.1.call-update) | async-done | bytes 8388624 | tf_op jit(solution)/shard_map/all_gather | solution.py:174
  227.1 6.4 convolution_bitcast_fusion
  234.8 2.9 fusion.72
  238.9 3.1 multiply_cosine_fusion
  241.9 6.3 fusion.121
  250.8 2.4 copy.75
  256.1 53.2 %all-gather.11.cloned.1.call-done = bf16[16384,2,128]{0,2,1:T(8,128)(2,1)} async-done(((bf16[1024,2,128]{0,2,1:T(8,128)(2,1)}), bf16[16384,2,128]{0,2,1:T(8,128)(2,1)}) %all-gather.11.cloned.1.call-update) | async-done | bytes 8388624 | tf_op jit(solution)/shard_map/all_gather | solution.py:27
  309.3 5.8 fusion.118
  315.1 6.4 copy.71
  321.5 6.4 copy.72
  327.9 285.7 %while.20 = (s32[]{:T(128)}, f32[1,2,1024]{2,1,0:T(2,128)S(1)}, f32[1,2,1024]{2,1,0:T(2,128)S(1)}, f32[1,2,1024,128]{3,2,1,0:T(8,128)}, s32[16]{0:T(128)S(1)}, /...) while((s32[]{:T(128)}, f32[1,2,1024]{2,1,0:T(2,128)S(1)}, ...), condition=%wide.region_12.13_spmd.clone, body=%wide.region_9.12_spmd.clone.sunk | while | flops 1102912512 | bytes 66208936 | solution.py:245
  329.8 6.2 fusion.145
  336.0 7.2 %fusion.148 = f32[1,2,1024,128]{3,2,1,0:T(8,128)} fusion(f32[1024,1024,2]{1,0,2:T(8,128)} %get-tuple-element.376, f32[2,1024]{1,0:T(2,128)S(1)} %bitcast.180, pred[1024,1024]{0,1:T(8,128)(4,1)S(1)} %broadcast_compare_fusion.2, f32[1,2,1024,128]{3,2,1,0:T(8,128)} %get-tuple-element.392, f32[2,1024]{1,0:T(2,128)S(1)} %get-tuple-element.377, ...), kind=kOutput, calls=%fused_computation.16.clone.1 | convolution fusion | flops 548143104 | bytes 11813377 | tf_op jit(solution)/shard_map/while/body/eval_jaxpr/kgqn,nkd->kgqd/dot_general | solution.py:237
  343.2 2.2 fusion.147
  347.3 6.2 fusion.145
  353.5 7.5 %fusion.148 = f32[1,2,1024,128]{3,2,1,0:T(8,128)} fusion(f32[1024,1024,2]{1,0,2:T(8,128)} %get-tuple-element.376, f32[2,1024]{1,0:T(2,128)S(1)} %bitcast.180, pred[1024,1024]{0,1:T(8,128)(4,1)S(1)} %broadcast_compare_fusion.2, f32[1,2,1024,128]{3,2,1,0:T(8,128)} %get-tuple-element.392, f32[2,1024]{1,0:T(2,128)S(1)} %get-tuple-element.377, ...), kind=kOutput, calls=%fused_computation.16.clone.1 | convolution fusion | flops 548143104 | bytes 11813377 | tf_op jit(solution)/shard_map/while/body/eval_jaxpr/kgqn,nkd->kgqd/dot_general | solution.py:237
  361.1 2.2 fusion.147
  365.2 6.2 fusion.145
  371.4 7.5 %fusion.148 = f32[1,2,1024,128]{3,2,1,0:T(8,128)} fusion(f32[1024,1024,2]{1,0,2:T(8,128)} %get-tuple-element.376, f32[2,1024]{1,0:T(2,128)S(1)} %bitcast.180, pred[1024,1024]{0,1:T(8,128)(4,1)S(1)} %broadcast_compare_fusion.2, f32[1,2,1024,128]{3,2,1,0:T(8,128)} %get-tuple-element.392, f32[2,1024]{1,0:T(2,128)S(1)} %get-tuple-element.377, ...), kind=kOutput, calls=%fused_computation.16.clone.1 | convolution fusion | flops 548143104 | bytes 11813377 | tf_op jit(solution)/shard_map/while/body/eval_jaxpr/kgqn,nkd->kgqd/dot_general | solution.py:237
  378.9 2.2 fusion.147
  383.0 6.2 fusion.145
  389.2 7.5 %fusion.148 = f32[1,2,1024,128]{3,2,1,0:T(8,128)} fusion(f32[1024,1024,2]{1,0,2:T(8,128)} %get-tuple-element.376, f32[2,1024]{1,0:T(2,128)S(1)} %bitcast.180, pred[1024,1024]{0,1:T(8,128)(4,1)S(1)} %broadcast_compare_fusion.2, f32[1,2,1024,128]{3,2,1,0:T(8,128)} %get-tuple-element.392, f32[2,1024]{1,0:T(2,128)S(1)} %get-tuple-element.377, ...), kind=kOutput, calls=%fused_computation.16.clone.1 | convolution fusion | flops 548143104 | bytes 11813377 | tf_op jit(solution)/shard_map/while/body/eval_jaxpr/kgqn,nkd->kgqd/dot_general | solution.py:237
  400.9 6.2 fusion.145
  407.1 7.5 %fusion.148 = f32[1,2,1024,128]{3,2,1,0:T(8,128)} fusion(f32[1024,1024,2]{1,0,2:T(8,128)} %get-tuple-element.376, f32[2,1024]{1,0:T(2,128)S(1)} %bitcast.180, pred[1024,1024]{0,1:T(8,128)(4,1)S(1)} %broadcast_compare_fusion.2, f32[1,2,1024,128]{3,2,1,0:T(8,128)} %get-tuple-element.392, f32[2,1024]{1,0:T(2,128)S(1)} %get-tuple-element.377, ...), kind=kOutput, calls=%fused_computation.16.clone.1 | convolution fusion | flops 548143104 | bytes 11813377 | tf_op jit(solution)/shard_map/while/body/eval_jaxpr/kgqn,nkd->kgqd/dot_general | solution.py:237
  414.7 2.2 fusion.147
  418.8 6.2 fusion.145
  425.0 7.5 %fusion.148 = f32[1,2,1024,128]{3,2,1,0:T(8,128)} fusion(f32[1024,1024,2]{1,0,2:T(8,128)} %get-tuple-element.376, f32[2,1024]{1,0:T(2,128)S(1)} %bitcast.180, pred[1024,1024]{0,1:T(8,128)(4,1)S(1)} %broadcast_compare_fusion.2, f32[1,2,1024,128]{3,2,1,0:T(8,128)} %get-tuple-element.392, f32[2,1024]{1,0:T(2,128)S(1)} %get-tuple-element.377, ...), kind=kOutput, calls=%fused_computation.16.clone.1 | convolution fusion | flops 548143104 | bytes 11813377 | tf_op jit(solution)/shard_map/while/body/eval_jaxpr/kgqn,nkd->kgqd/dot_general | solution.py:237
  432.5 2.2 fusion.147
  436.6 6.2 fusion.145
  442.8 7.5 %fusion.148 = f32[1,2,1024,128]{3,2,1,0:T(8,128)} fusion(f32[1024,1024,2]{1,0,2:T(8,128)} %get-tuple-element.376, f32[2,1024]{1,0:T(2,128)S(1)} %bitcast.180, pred[1024,1024]{0,1:T(8,128)(4,1)S(1)} %broadcast_compare_fusion.2, f32[1,2,1024,128]{3,2,1,0:T(8,128)} %get-tuple-element.392, f32[2,1024]{1,0:T(2,128)S(1)} %get-tuple-element.377, ...), kind=kOutput, calls=%fused_computation.16.clone.1 | convolution fusion | flops 548143104 | bytes 11813377 | tf_op jit(solution)/shard_map/while/body/eval_jaxpr/kgqn,nkd->kgqd/dot_general | solution.py:237
  454.5 6.2 fusion.145
  460.7 7.5 %fusion.148 = f32[1,2,1024,128]{3,2,1,0:T(8,128)} fusion(f32[1024,1024,2]{1,0,2:T(8,128)} %get-tuple-element.376, f32[2,1024]{1,0:T(2,128)S(1)} %bitcast.180, pred[1024,1024]{0,1:T(8,128)(4,1)S(1)} %broadcast_compare_fusion.2, f32[1,2,1024,128]{3,2,1,0:T(8,128)} %get-tuple-element.392, f32[2,1024]{1,0:T(2,128)S(1)} %get-tuple-element.377, ...), kind=kOutput, calls=%fused_computation.16.clone.1 | convolution fusion | flops 548143104 | bytes 11813377 | tf_op jit(solution)/shard_map/while/body/eval_jaxpr/kgqn,nkd->kgqd/dot_general | solution.py:237
  468.2 2.2 fusion.147
  472.4 6.2 fusion.145
  478.5 7.5 %fusion.148 = f32[1,2,1024,128]{3,2,1,0:T(8,128)} fusion(f32[1024,1024,2]{1,0,2:T(8,128)} %get-tuple-element.376, f32[2,1024]{1,0:T(2,128)S(1)} %bitcast.180, pred[1024,1024]{0,1:T(8,128)(4,1)S(1)} %broadcast_compare_fusion.2, f32[1,2,1024,128]{3,2,1,0:T(8,128)} %get-tuple-element.392, f32[2,1024]{1,0:T(2,128)S(1)} %get-tuple-element.377, ...), kind=kOutput, calls=%fused_computation.16.clone.1 | convolution fusion | flops 548143104 | bytes 11813377 | tf_op jit(solution)/shard_map/while/body/eval_jaxpr/kgqn,nkd->kgqd/dot_general | solution.py:237
  490.2 6.2 fusion.145
  496.4 7.5 %fusion.148 = f32[1,2,1024,128]{3,2,1,0:T(8,128)} fusion(f32[1024,1024,2]{1,0,2:T(8,128)} %get-tuple-element.376, f32[2,1024]{1,0:T(2,128)S(1)} %bitcast.180, pred[1024,1024]{0,1:T(8,128)(4,1)S(1)} %broadcast_compare_fusion.2, f32[1,2,1024,128]{3,2,1,0:T(8,128)} %get-tuple-element.392, f32[2,1024]{1,0:T(2,128)S(1)} %get-tuple-element.377, ...), kind=kOutput, calls=%fused_computation.16.clone.1 | convolution fusion | flops 548143104 | bytes 11813377 | tf_op jit(solution)/shard_map/while/body/eval_jaxpr/kgqn,nkd->kgqd/dot_general | solution.py:237
  508.1 6.2 fusion.145
  514.3 7.5 %fusion.148 = f32[1,2,1024,128]{3,2,1,0:T(8,128)} fusion(f32[1024,1024,2]{1,0,2:T(8,128)} %get-tuple-element.376, f32[2,1024]{1,0:T(2,128)S(1)} %bitcast.180, pred[1024,1024]{0,1:T(8,128)(4,1)S(1)} %broadcast_compare_fusion.2, f32[1,2,1024,128]{3,2,1,0:T(8,128)} %get-tuple-element.392, f32[2,1024]{1,0:T(2,128)S(1)} %get-tuple-element.377, ...), kind=kOutput, calls=%fused_computation.16.clone.1 | convolution fusion | flops 548143104 | bytes 11813377 | tf_op jit(solution)/shard_map/while/body/eval_jaxpr/kgqn,nkd->kgqd/dot_general | solution.py:237
  521.8 2.2 fusion.147
  525.9 6.2 fusion.145
  532.1 7.5 %fusion.148 = f32[1,2,1024,128]{3,2,1,0:T(8,128)} fusion(f32[1024,1024,2]{1,0,2:T(8,128)} %get-tuple-element.376, f32[2,1024]{1,0:T(2,128)S(1)} %bitcast.180, pred[1024,1024]{0,1:T(8,128)(4,1)S(1)} %broadcast_compare_fusion.2, f32[1,2,1024,128]{3,2,1,0:T(8,128)} %get-tuple-element.392, f32[2,1024]{1,0:T(2,128)S(1)} %get-tuple-element.377, ...), kind=kOutput, calls=%fused_computation.16.clone.1 | convolution fusion | flops 548143104 | bytes 11813377 | tf_op jit(solution)/shard_map/while/body/eval_jaxpr/kgqn,nkd->kgqd/dot_general | solution.py:237
  543.8 6.2 fusion.145
  550.0 7.5 %fusion.148 = f32[1,2,1024,128]{3,2,1,0:T(8,128)} fusion(f32[1024,1024,2]{1,0,2:T(8,128)} %get-tuple-element.376, f32[2,1024]{1,0:T(2,128)S(1)} %bitcast.180, pred[1024,1024]{0,1:T(8,128)(4,1)S(1)} %broadcast_compare_fusion.2, f32[1,2,1024,128]{3,2,1,0:T(8,128)} %get-tuple-element.392, f32[2,1024]{1,0:T(2,128)S(1)} %get-tuple-element.377, ...), kind=kOutput, calls=%fused_computation.16.clone.1 | convolution fusion | flops 548143104 | bytes 11813377 | tf_op jit(solution)/shard_map/while/body/eval_jaxpr/kgqn,nkd->kgqd/dot_general | solution.py:237
  561.7 6.2 fusion.145
  567.9 7.5 %fusion.148 = f32[1,2,1024,128]{3,2,1,0:T(8,128)} fusion(f32[1024,1024,2]{1,0,2:T(8,128)} %get-tuple-element.376, f32[2,1024]{1,0:T(2,128)S(1)} %bitcast.180, pred[1024,1024]{0,1:T(8,128)(4,1)S(1)} %broadcast_compare_fusion.2, f32[1,2,1024,128]{3,2,1,0:T(8,128)} %get-tuple-element.392, f32[2,1024]{1,0:T(2,128)S(1)} %get-tuple-element.377, ...), kind=kOutput, calls=%fused_computation.16.clone.1 | convolution fusion | flops 548143104 | bytes 11813377 | tf_op jit(solution)/shard_map/while/body/eval_jaxpr/kgqn,nkd->kgqd/dot_general | solution.py:237
  575.4 2.2 fusion.147
  579.5 6.2 fusion.145
  585.7 7.5 %fusion.148 = f32[1,2,1024,128]{3,2,1,0:T(8,128)} fusion(f32[1024,1024,2]{1,0,2:T(8,128)} %get-tuple-element.376, f32[2,1024]{1,0:T(2,128)S(1)} %bitcast.180, pred[1024,1024]{0,1:T(8,128)(4,1)S(1)} %broadcast_compare_fusion.2, f32[1,2,1024,128]{3,2,1,0:T(8,128)} %get-tuple-element.392, f32[2,1024]{1,0:T(2,128)S(1)} %get-tuple-element.377, ...), kind=kOutput, calls=%fused_computation.16.clone.1 | convolution fusion | flops 548143104 | bytes 11813377 | tf_op jit(solution)/shard_map/while/body/eval_jaxpr/kgqn,nkd->kgqd/dot_general | solution.py:237
  597.4 6.2 fusion.145
  603.6 7.5 %fusion.148 = f32[1,2,1024,128]{3,2,1,0:T(8,128)} fusion(f32[1024,1024,2]{1,0,2:T(8,128)} %get-tuple-element.376, f32[2,1024]{1,0:T(2,128)S(1)} %bitcast.180, pred[1024,1024]{0,1:T(8,128)(4,1)S(1)} %broadcast_compare_fusion.2, f32[1,2,1024,128]{3,2,1,0:T(8,128)} %get-tuple-element.392, f32[2,1024]{1,0:T(2,128)S(1)} %get-tuple-element.377, ...), kind=kOutput, calls=%fused_computation.16.clone.1 | convolution fusion | flops 548143104 | bytes 11813377 | tf_op jit(solution)/shard_map/while/body/eval_jaxpr/kgqn,nkd->kgqd/dot_general | solution.py:237
  611.1 2.2 fusion.147
  615.4 5.6 convolution_convert_fusion
  621.0 51.8 %reduce-scatter.2.cloned.1.call-done = bf16[128,4096]{1,0:T(8,128)(2,1)} async-done(((bf16[1024,4096]{1,0:T(8,128)(2,1)}), bf16[128,4096]{1,0:T(8,128)(2,1)}) %reduce-scatter.2.cloned.1.call-update) | async-done | bytes 1048592 | tf_op jit(solution)/shard_map/reduce_scatter | solution.py:249
  (219 shorter events, 83.9 us)
Async XLA Ops:
  6.5 608.8 %copy-start = (bf16[256,4096]{1,0:T(8,128)(2,1)S(1)}, bf16[256,4096]{1,0:T(8,128)(2,1)}, u32[]{:S(2)}) copy-start(bf16[256,4096]{1,0:T(8,128)(2,1)} %param.37) | copy-start | bytes 6291460
  6.5 83.5 %copy-start.9 = (f32[1280]{0:T(1024)S(1)}, f32[1280]{0:T(1024)}, u32[]{:S(2)}) copy-start(f32[1280]{0:T(1024)} %param.25) | copy-start | bytes 15364
  6.5 83.5 %copy-start.8 = (f32[1280]{0:T(1024)S(1)}, f32[1280]{0:T(1024)}, u32[]{:S(2)}) copy-start(f32[1280]{0:T(1024)} %param.26) | copy-start | bytes 15364
  6.5 83.5 %copy-start.7 = (f32[3840]{0:T(1024)S(1)}, f32[3840]{0:T(1024)}, u32[]{:S(2)}) copy-start(f32[3840]{0:T(1024)} %param.28) | copy-start | bytes 46084
  6.5 83.5 %all-gather.5.cloned.1.call-start = ((), (), s32[]{:S(2)}) async-start(), calls=%async_computation.2 | async-start | bytes 10444800 | tf_op jit(solution)/shard_map/all_gather | solution.py:122
  7.3 132.6 %all-gather.7.cloned.1.call-start = ((), (), s32[]{:S(2)}) async-start(), calls=%async_computation.3 | async-start | bytes 3481600 | tf_op jit(solution)/shard_map/all_gather | solution.py:138
  8.0 19.3 %collective-permute-start = (bf16[2,256,1280]{2,1,0:T(8,128)(2,1)}, bf16[2,256,1280]{2,1,0:T(8,128)(2,1)}, u32[]{:S(2)}, u32[]{:S(2)}) collective-permute-start(bf16[2,256,1280]{2,1,0:T(8,128)(2,1)} %param.20), channel_id=1, source_target_pairs={{0,16},{16,0},{32,48},{48,32},{64,80},{80,64},{96,112},{112,96},{1... | collective-permute-start | bytes 3932168 | tf_op jit(solution)/shard_map/ppermute | solution.py:21
  105.7 34.2 %copy-start.10 = (f32[1280]{0:T(1024)S(1)}, f32[1280]{0:T(1024)}, u32[]{:S(2)}) copy-start(f32[1280]{0:T(1024)} %param.30) | copy-start | bytes 15364
  150.6 22.8 %copy-start.5 = (f32[4096]{0:T(1024)S(1)}, f32[4096]{0:T(1024)}, u32[]{:S(2)}) copy-start(f32[4096]{0:T(1024)} %param.32) | copy-start | bytes 49156
  152.9 19.3 %all-to-all-start = ((bf16[128,2,640]{2,1,0:T(2,128)(2,1)}), bf16[128,2,640]{2,1,0:T(2,128)(2,1)S(1)}, u32[]{:S(2)}, u32[]{:S(2)}) async-start(bf16[128,2,640]{2,1,0:T(2,128)(2,1)} %reshape.851), calls=%async_computation | async-start | bytes 655360 | tf_op jit(solution)/shard_map/all_to_all | solution.py:153
  160.4 66.8 %all-gather.9.cloned.1.call-start = ((), (), s32[]{:S(2)}) async-start(), calls=%async_computation.4 | async-start | bytes 9437184 | tf_op jit(solution)/shard_map/all_gather | solution.py:174
  173.5 6.3 copy-start.6
  179.7 47.4 %copy-start.3 = (bf16[4096,128]{1,0:T(8,128)(2,1)S(1)}, bf16[4096,128]{1,0:T(8,128)(2,1)}, u32[]{:S(2)}) copy-start(bf16[4096,128]{1,0:T(8,128)(2,1)} %param.35) | copy-start | bytes 3145732
  181.0 128.2 %all-gather.11.cloned.1.call-start = ((), (), s32[]{:S(2)}) async-start(), calls=%async_computation.5 | async-start | bytes 8912896 | tf_op jit(solution)/shard_map/all_gather | solution.py:27
  227.1 7.6 %copy-start.2 = (bf16[1024,4096]{1,0:T(8,128)(2,1)S(1)}, bf16[1024,4096]{1,0:T(8,128)(2,1)}, u32[]{:S(2)}) copy-start(bf16[1024,4096]{1,0:T(8,128)(2,1)} %all-gather.9.cloned.1.call-done) | copy-start | bytes 25165828
  227.1 7.6 %copy-start.4 = (bf16[4096,128]{1,0:T(8,128)(2,1)S(1)}, bf16[4096,128]{1,0:T(8,128)(2,1)}, u32[]{:S(2)}) copy-start(bf16[4096,128]{1,0:T(8,128)(2,1)} %param.36) | copy-start | bytes 3145732
  238.6 434.2 %reduce-scatter.2.cloned.1.call-start = ((), (), s32[]{:S(2)}) async-start(), calls=%async_computation.6 | async-start | bytes 9437184 | tf_op jit(solution)/shard_map/reduce_scatter | solution.py:249
  336.0 7.3 %copy-start.1 = (f32[1024,1024,2]{1,0,2:T(8,128)S(1)}, f32[1024,1024,2]{1,0,2:T(8,128)}, u32[]{:S(2)}) copy-start(f32[1024,1024,2]{1,0,2:T(8,128)} %get-tuple-element.376) | copy-start | bytes 25165828 | tf_op jit(solution)/shard_map/while
  353.5 7.6 %copy-start.1 = (f32[1024,1024,2]{1,0,2:T(8,128)S(1)}, f32[1024,1024,2]{1,0,2:T(8,128)}, u32[]{:S(2)}) copy-start(f32[1024,1024,2]{1,0,2:T(8,128)} %get-tuple-element.376) | copy-start | bytes 25165828 | tf_op jit(solution)/shard_map/while
  371.4 7.6 %copy-start.1 = (f32[1024,1024,2]{1,0,2:T(8,128)S(1)}, f32[1024,1024,2]{1,0,2:T(8,128)}, u32[]{:S(2)}) copy-start(f32[1024,1024,2]{1,0,2:T(8,128)} %get-tuple-element.376) | copy-start | bytes 25165828 | tf_op jit(solution)/shard_map/while
  389.2 7.6 %copy-start.1 = (f32[1024,1024,2]{1,0,2:T(8,128)S(1)}, f32[1024,1024,2]{1,0,2:T(8,128)}, u32[]{:S(2)}) copy-start(f32[1024,1024,2]{1,0,2:T(8,128)} %get-tuple-element.376) | copy-start | bytes 25165828 | tf_op jit(solution)/shard_map/while
  407.1 7.6 %copy-start.1 = (f32[1024,1024,2]{1,0,2:T(8,128)S(1)}, f32[1024,1024,2]{1,0,2:T(8,128)}, u32[]{:S(2)}) copy-start(f32[1024,1024,2]{1,0,2:T(8,128)} %get-tuple-element.376) | copy-start | bytes 25165828 | tf_op jit(solution)/shard_map/while
  425.0 7.6 %copy-start.1 = (f32[1024,1024,2]{1,0,2:T(8,128)S(1)}, f32[1024,1024,2]{1,0,2:T(8,128)}, u32[]{:S(2)}) copy-start(f32[1024,1024,2]{1,0,2:T(8,128)} %get-tuple-element.376) | copy-start | bytes 25165828 | tf_op jit(solution)/shard_map/while
  442.8 7.6 %copy-start.1 = (f32[1024,1024,2]{1,0,2:T(8,128)S(1)}, f32[1024,1024,2]{1,0,2:T(8,128)}, u32[]{:S(2)}) copy-start(f32[1024,1024,2]{1,0,2:T(8,128)} %get-tuple-element.376) | copy-start | bytes 25165828 | tf_op jit(solution)/shard_map/while
  460.7 7.6 %copy-start.1 = (f32[1024,1024,2]{1,0,2:T(8,128)S(1)}, f32[1024,1024,2]{1,0,2:T(8,128)}, u32[]{:S(2)}) copy-start(f32[1024,1024,2]{1,0,2:T(8,128)} %get-tuple-element.376) | copy-start | bytes 25165828 | tf_op jit(solution)/shard_map/while
  478.5 7.6 %copy-start.1 = (f32[1024,1024,2]{1,0,2:T(8,128)S(1)}, f32[1024,1024,2]{1,0,2:T(8,128)}, u32[]{:S(2)}) copy-start(f32[1024,1024,2]{1,0,2:T(8,128)} %get-tuple-element.376) | copy-start | bytes 25165828 | tf_op jit(solution)/shard_map/while
  496.4 7.6 %copy-start.1 = (f32[1024,1024,2]{1,0,2:T(8,128)S(1)}, f32[1024,1024,2]{1,0,2:T(8,128)}, u32[]{:S(2)}) copy-start(f32[1024,1024,2]{1,0,2:T(8,128)} %get-tuple-element.376) | copy-start | bytes 25165828 | tf_op jit(solution)/shard_map/while
  514.3 7.6 %copy-start.1 = (f32[1024,1024,2]{1,0,2:T(8,128)S(1)}, f32[1024,1024,2]{1,0,2:T(8,128)}, u32[]{:S(2)}) copy-start(f32[1024,1024,2]{1,0,2:T(8,128)} %get-tuple-element.376) | copy-start | bytes 25165828 | tf_op jit(solution)/shard_map/while
  532.1 7.6 %copy-start.1 = (f32[1024,1024,2]{1,0,2:T(8,128)S(1)}, f32[1024,1024,2]{1,0,2:T(8,128)}, u32[]{:S(2)}) copy-start(f32[1024,1024,2]{1,0,2:T(8,128)} %get-tuple-element.376) | copy-start | bytes 25165828 | tf_op jit(solution)/shard_map/while
  550.0 7.6 %copy-start.1 = (f32[1024,1024,2]{1,0,2:T(8,128)S(1)}, f32[1024,1024,2]{1,0,2:T(8,128)}, u32[]{:S(2)}) copy-start(f32[1024,1024,2]{1,0,2:T(8,128)} %get-tuple-element.376) | copy-start | bytes 25165828 | tf_op jit(solution)/shard_map/while
  567.8 7.6 %copy-start.1 = (f32[1024,1024,2]{1,0,2:T(8,128)S(1)}, f32[1024,1024,2]{1,0,2:T(8,128)}, u32[]{:S(2)}) copy-start(f32[1024,1024,2]{1,0,2:T(8,128)} %get-tuple-element.376) | copy-start | bytes 25165828 | tf_op jit(solution)/shard_map/while
  585.7 7.6 %copy-start.1 = (f32[1024,1024,2]{1,0,2:T(8,128)S(1)}, f32[1024,1024,2]{1,0,2:T(8,128)}, u32[]{:S(2)}) copy-start(f32[1024,1024,2]{1,0,2:T(8,128)} %get-tuple-element.376) | copy-start | bytes 25165828 | tf_op jit(solution)/shard_map/while
  603.6 7.6 %copy-start.1 = (f32[1024,1024,2]{1,0,2:T(8,128)S(1)}, f32[1024,1024,2]{1,0,2:T(8,128)}, u32[]{:S(2)}) copy-start(f32[1024,1024,2]{1,0,2:T(8,128)} %get-tuple-element.376) | copy-start | bytes 25165828 | tf_op jit(solution)/shard_map/while
Sparse Core Ops, SparseCore 0:
  9.5 80.4 all-gather.4
  92.3 47.5 all-gather.6
  181.2 45.9 all-gather.8
  238.7 70.5 all-gather.10
  621.1 51.6 reduce-scatter.1
where the time goes:
time: 681 us; the launch traced here: 679 us
  matrix products  263 us (39%)
  waiting for transfers between devices  256 us (38%)
  other arithmetic  76.8 us (11%)
  local copies, waits for them, and re-layouts  52.4 us (8%)
  between operations  20.1 us (3%)
  starting transfers between devices  9.5 us (1%)
    dot_general x16, matrix products, visit(): jnp.einsum('kgqn,nkd->kgqd', expd.astype(jnp.bfloat16), value_block, pref...  120 us
    dot_general x16, matrix products, visit(): jnp.einsum('qkgd,nkd->kgqn', grouped_rows, key_block, preferred_element_t...  98.7 us
    all_gather x1, waiting for transfers between devices, per_device(): lax.all_gather(vit_qkv_w, 'seq', axis=0, tiled=True)  60.5 us
    all_gather x1, waiting for transfers between devices, in_one_piece(): result = lax.all_gather(both, axis, axis=dim, tiled=True)  53.2 us
    reduce_scatter x1, waiting for transfers between devices, per_device(): lax.psum_scatter(jnp.dot(context_tok, wo, preferred_element_type=jnp.floa...  51.8 us
    all_gather x1, waiting for transfers between devices, per_device(): shard_piece = lax.all_gather(normed_tok, 'frame', axis=0, tiled=True)  46 us
    reduce_sum x16, other arithmetic, visit(): denominator = denominator * rescale + jnp.sum(expd, axis=-1)  35.8 us
    all_gather x1, waiting for transfers between devices, per_device(): lax.all_gather(vit_out_w, 'seq', axis=0, tiled=True)  31.7 us
  transfers between devices with their start and end apart: 7, of which 6 were waited for; matrix products, arithmetic and copies ran while one was open for 7% of the time, Pallas kernels for 0%

commit v1 on v0

--- a/solution.py
+++ b/solution.py
@@ -3,6 +3,8 @@
 import jax
 import jax.numpy as jnp
 from jax import lax
+from jax.experimental import pallas as pl
+from jax.experimental.pallas import tpu as pltpu
 from jax.sharding import PartitionSpec as P
 
 VHEADS = 16
@@ -21,11 +23,78 @@
     return lax.ppermute(value, axis, pairs)
 
 
-def in_one_piece(arrays, axis, dim, along):
-    widths = [a.shape[along] for a in arrays]
-    both = jnp.concatenate(arrays, axis=along)
-    result = lax.all_gather(both, axis, axis=dim, tiled=True)
-    return tuple(jnp.split(result, [sum(widths[:k]) for k in range(1, len(widths))], axis=along))
+T_TILE = 16
+
+
+def attend_kernel(seq_ref, q_ref, kv_ref, out_ref):
+    tile = pl.program_id(0)
+    my_seq = seq_ref[0]
+    slots = q_ref.shape[0]
+    groups = kv_ref.shape[0]
+    rows = slots * T_TILE
+    wide = q_ref[...].reshape(rows, 2 * HEAD_WIDTH)
+    q = jnp.concatenate([wide[:, :HEAD_WIDTH], wide[:, HEAD_WIDTH:]], axis=0)
+    keys_n = groups * T_TILE
+    chunk = 1024
+    state = (
+        jnp.full((2 * rows, 1), masked_score, jnp.float32),
+        jnp.zeros((2 * rows, 2 * HEAD_WIDTH), jnp.float32),
+    )
+    ones = jnp.ones((chunk, HEAD_WIDTH), jnp.bfloat16)
+
+    def block(j, state, diagonal):
+        kv = kv_ref[:, pl.ds(pl.multiple_of(j * T_TILE, T_TILE), T_TILE), :].reshape(
+            keys_n, 2 * HEAD_WIDTH
+        )
+        scores = []
+        for c in range(keys_n // chunk):
+            part = kv[c * chunk : (c + 1) * chunk, :HEAD_WIDTH]
+            scores.append(
+                lax.dot_general(
+                    q, part, (((1,), (1,)), ((), ())), preferred_element_type=jnp.float32
+                )
+            )
+        high, acc = state
+        for c in range(keys_n // chunk):
+            score = scores[c]
+            if diagonal:
+                row = lax.broadcasted_iota(jnp.int32, (2 * rows, 1), 0) % rows
+                row_pos = row % T_TILE * 128 + row // T_TILE * 16 + my_seq
+                col = lax.broadcasted_iota(jnp.int32, (1, chunk), 1) + c * chunk
+                group = col // T_TILE
+                col_pos = col % T_TILE * 128 + group % slots * 16 + group // slots
+                score = jnp.where(col_pos <= row_pos, score, masked_score)
+            new_high = jnp.maximum(high, jnp.max(score, axis=1, keepdims=True))
+            e = jnp.exp2(score - new_high).astype(jnp.bfloat16)
+            values = jnp.concatenate([kv[c * chunk : (c + 1) * chunk, HEAD_WIDTH:], ones], axis=1)
+            acc = acc * jnp.exp2(high - new_high) + jnp.dot(
+                e, values, preferred_element_type=jnp.float32
+            )
+            high = new_high
+        return (high, acc)
+
+    state = block(tile, state, True)
+    state = lax.fori_loop(0, tile, lambda j, st: block(j, st, False), state)
+    acc = state[1]
+    context = (acc[:, :HEAD_WIDTH] / acc[:, HEAD_WIDTH:]).astype(jnp.bfloat16)
+    context = jnp.concatenate([context[:rows], context[rows:]], axis=1)
+    out_ref[...] = context.reshape(slots, T_TILE, 2 * HEAD_WIDTH)
+
+
+def attend(my_seq, q, kv):
+    slots, frames, width = q.shape
+    return pl.pallas_call(
+        attend_kernel,
+        grid=(frames // T_TILE,),
+        in_specs=[
+            pl.BlockSpec(memory_space=pltpu.SMEM),
+            pl.BlockSpec((slots, T_TILE, width), lambda i: (0, i, 0)),
+            pl.BlockSpec(memory_space=pltpu.VMEM),
+        ],
+        out_specs=pl.BlockSpec((slots, T_TILE, width), lambda i: (0, i, 0)),
+        out_shape=jax.ShapeDtypeStruct((slots, frames, width), jnp.bfloat16),
+        name="attend",
+    )(my_seq, q, kv)
 
 
 def apply_rotary(values, rotary_angles):
@@ -188,8 +257,11 @@
     row_ids = jnp.arange(group_rows)
     group_positions = row_ids % own_rows * devices_n + row_ids // own_rows * seqs_n + my_seq
     rotary_angles = rope_angles(group_positions, HEAD_WIDTH)[:, None, :]
-    query_matrix = apply_rotary(
-        projected[:, :query_width].reshape(group_rows, query_heads, HEAD_WIDTH), rotary_angles
+    query_matrix = (
+        apply_rotary(
+            projected[:, :query_width].reshape(group_rows, query_heads, HEAD_WIDTH), rotary_angles
+        )
+        * (math.log2(math.e) / math.sqrt(HEAD_WIDTH))
     ).astype(jnp.bfloat16)
     keys_own = apply_rotary(
         projected[:, query_width : query_width + kv_width].reshape(
@@ -202,50 +274,17 @@
         .astype(jnp.bfloat16)
         .reshape(group_rows, kv_heads, HEAD_WIDTH)
     )
-    grouped_rows = query_matrix.reshape(group_rows, kv_heads, query_heads // kv_heads, HEAD_WIDTH)
-    group_size = query_heads // kv_heads
-    start_state = (
-        jnp.full((kv_heads, group_size, group_rows), masked_score, jnp.float32),
-        jnp.zeros((kv_heads, group_size, group_rows), jnp.float32),
-        jnp.zeros((kv_heads, group_size, group_rows, HEAD_WIDTH), jnp.float32),
-    )
-    carry = start_state
-    key_piece, value_piece = in_one_piece((keys_own, values_own), "seq", 0, 1)
-    piece_rows = key_piece.shape[0]
-    inner_rows = math.gcd(piece_rows, 1024)
-    steps_n = piece_rows // inner_rows
-    key_blocks = key_piece.reshape(steps_n, inner_rows, kv_heads, HEAD_WIDTH)
-    value_blocks = value_piece.reshape(steps_n, inner_rows, kv_heads, HEAD_WIDTH)
-    block_offsets = inner_rows * jnp.arange(steps_n)
-
-    def visit(running, operands):
-        running_max, denominator, weighted = running
-        key_block, value_block, block_offset = operands
-        gathered_ids = block_offset + jnp.arange(inner_rows)
-        seq_of = gathered_ids // group_rows
-        inner_ids = gathered_ids % group_rows
-        key_positions = inner_ids % own_rows * devices_n + inner_ids // own_rows * seqs_n + seq_of
-        block_scores = jnp.einsum(
-            "qkgd,nkd->kgqn", grouped_rows, key_block, preferred_element_type=jnp.float32
-        ) / math.sqrt(HEAD_WIDTH)
-        allowed = key_positions[None, :] <= group_positions[:, None]
-        block_scores = jnp.where(allowed[None, None], block_scores, masked_score)
-        new_max = jnp.maximum(running_max, jnp.max(block_scores, axis=-1))
-        expd = jnp.where(allowed[None, None], jnp.exp(block_scores - new_max[..., None]), 0.0)
-        rescale = jnp.exp(running_max - new_max)
-        denominator = denominator * rescale + jnp.sum(expd, axis=-1)
-        weighted = weighted * rescale[..., None] + jnp.einsum(
-            "kgqn,nkd->kgqd",
-            expd.astype(jnp.bfloat16),
-            value_block,
-            preferred_element_type=jnp.float32,
-        )
-        return ((new_max, denominator, weighted), None)
-
-    carry, unused = lax.scan(visit, carry, (key_blocks, value_blocks, block_offsets))
-    final_max, denominator, weighted = carry
-    context_tok = (weighted / denominator[..., None]).astype(jnp.bfloat16)
-    context_tok = jnp.transpose(context_tok, (2, 0, 1, 3)).reshape(group_rows, query_width)
+    kv_own = jnp.concatenate(
+        [keys_own.reshape(group_rows, kv_width), values_own.reshape(group_rows, kv_width)], axis=1
+    )
+    kv_all = lax.all_gather(kv_own, "seq", axis=0, tiled=True).reshape(
+        seqs_n * frames_n, own_rows, 2 * kv_width
+    )
+    context_tok = attend(
+        my_seq.reshape(1).astype(jnp.int32),
+        query_matrix.reshape(frames_n, own_rows, query_width),
+        kv_all,
+    ).reshape(group_rows, query_width)
     summed = lax.psum_scatter(
         jnp.dot(context_tok, wo, preferred_element_type=jnp.float32).astype(jnp.bfloat16),
         "frame",

time: 681 us -> 425 us (0.62)
  matrix products: 263 us -> 45.2 us
  other arithmetic: 76.8 us -> 21.8 us
  Pallas kernels: 0 us -> 38.3 us
  local copies, waits for them, and re-layouts: 52.4 us -> 34.8 us
    dot_general x32 -> x0, matrix products: 219 us -> none  [the longest x16 120 us: visit(): jnp.einsum('kgqn,nkd->kgqd', expd.astype(jnp.bfloat16), value_block, pref...]
    pallas_call x0 -> x1, Pallas kernels: none -> 38.3 us  [attend(): pl.pallas_call(attend_kernel, grid=(frames // T_TILE,), in_specs=[pl.Bloc...]
    reduce_sum x16 -> x0, other arithmetic: 35.8 us -> none  [visit(): denominator = denominator * rescale + jnp.sum(expd, axis=-1)]
    unnamed x27 -> x25, local copies, waits for them, and re-layouts: 17.8 us -> 4.82 us
    all_gather x0 -> x1, local copies, waits for them, and re-layouts: none -> 11.9 us  [per_device(): lax.all_gather(kv_own, 'seq', axis=0, tiled=True)]
    le x16 -> x0, other arithmetic: 10.4 us -> none  [visit(): allowed = key_positions[None, :] <= group_positions[:, None]]
    add x32 -> x0, other arithmetic: 9.68 us -> none  [the longest x16 9.25 us: visit(): inner_ids % own_rows * devices_n + inner_ids // own_rows * seqs_n + seq_of]
    dynamic_slice x16 -> x0, local copies, waits for them, and re-layouts: 9.26 us -> none  [per_device(): lax.scan(visit, carry, (key_blocks, value_blocks, block_offsets))]
  transfers between devices with their start and end apart: 7 -> 7, of which waited for: 6 -> 6; matrix products, arithmetic and copies ran while one was open for 7% -> 12% of each run, Pallas kernels for 0% -> 0%
where the time goes in v1:
time: 425 us; the launch traced here: 424 us
  waiting for transfers between devices  254 us (60%)
  matrix products  45.2 us (11%)
  Pallas kernels  38.3 us (9%)
  local copies, waits for them, and re-layouts  34.8 us (8%)
  other arithmetic  21.8 us (5%)
  between operations  20 us (5%)
  starting transfers between devices  9.47 us (2%)
    all_gather x1, waiting for transfers between devices, per_device(): lax.all_gather(vit_qkv_w, 'seq', axis=0, tiled=True)  60.3 us
    reduce_scatter x1, waiting for transfers between devices, per_device(): lax.psum_scatter(jnp.dot(context_tok, wo, preferred_element_type=jnp.floa...  51.8 us
    all_gather x1, waiting for transfers between devices, per_device(): lax.all_gather(kv_own, 'seq', axis=0, tiled=True)  51.5 us
    all_gather x1, waiting for transfers between devices, per_device(): shard_piece = lax.all_gather(normed_tok, 'frame', axis=0, tiled=True)  46 us
    pallas_call x1, Pallas kernels, attend(): pl.pallas_call(attend_kernel, grid=(frames // T_TILE,), in_specs=[pl.Bloc...  38.3 us
    all_gather x1, waiting for transfers between devices, per_device(): lax.all_gather(vit_out_w, 'seq', axis=0, tiled=True)  31.7 us
    dot_general x2, matrix products, add_columns(): return jnp.dot(left, shard_piece, preferred_element_type=jnp.float32)  12.1 us
    all_gather x1, local copies, waits for them, and re-layouts, per_device(): lax.all_gather(kv_own, 'seq', axis=0, tiled=True)  11.9 us
  transfers between devices with their start and end apart: 7, of which 6 were waited for; matrix products, arithmetic and copies ran while one was open for 12% of the time, Pallas kernels for 0%

profile of v1, /device:TPU:1, one launch (start us, length us, event | category | flops | bytes accessed | tf_op | source)
XLA Modules:
  0.0 424.0 jit_solution(8355540121842797190)
XLA Ops:
  6.5 0.7 all-gather.5.cloned.1.call-update
  7.3 0.0 all-gather.7.cloned.1.call-start
  7.3 0.7 all-gather.7.cloned.1.call-update
  8.0 1.5 collective-permute-start
  9.5 0.7 and_select_fusion.6
  10.2 0.7 fusion.55
  10.8 0.2 convert_reduce_fusion.1
  11.0 0.7 select_reduce_fusion.1
  13.7 1.3 dynamic-slice.5
  14.9 1.3 dynamic-slice.4
  16.3 1.6 gather_fusion.1
  17.9 1.6 gather_fusion
  23.4 1.2 gather_fusion.3
  25.4 0.6 iota_compare_fusion
  26.0 0.7 compare_select_fusion.1
  26.7 0.7 compare_and_fusion.1
  27.5 1.9 convert_reduce_fusion
  29.4 0.3 fusion.17
  29.7 60.3 %all-gather.5.cloned.1.call-done = bf16[1280,3840]{1,0:T(8,128)(2,1)} async-done(((bf16[80,3840]{1,0:T(8,128)(2,1)}), bf16[1280,3840]{1,0:T(8,128)(2,1)}) %all-gather.5.cloned.1.call-update) | async-done | bytes 9830416 | tf_op jit(solution)/shard_map/all_gather | solution.py:191
  90.1 7.9 %fusion.1 = bf16[256,3840]{1,0:T(8,128)(2,1)} fusion(bf16[1280,3840]{1,0:T(8,128)(2,1)} %all-gather.5.cloned.1.call-done, f32[3840]{0:T(1024)S(1)} %copy-done.6, bf16[1,256,1280]{2,1,0:T(8,128)(2,1)S(1)} %get-tuple-element.30, f32[1280]{0:T(1024)S(1)} %copy-done.7, f32[1280]{0:T(1024)S(1)} %copy-done.8, f32[256]{0:T(256)S(1)} %add_rsqrt_fusion, ...), kind=kOutput, calls=%fused_computation.8 | convolution fusion | flops 2520514560 | bytes 12479488 | tf_op jit(solution)/shard_map/dot_general | solution.py:122
  97.9 4.0 copy.43
  101.9 2.1 fusion.26
  104.0 1.7 fusion.68
  105.8 2.4 fusion.16
  108.2 31.7 %all-gather.7.cloned.1.call-done = bf16[1280,1280]{1,0:T(8,128)(2,1)} async-done(((bf16[80,1280]{1,0:T(8,128)(2,1)}), bf16[1280,1280]{1,0:T(8,128)(2,1)}) %all-gather.7.cloned.1.call-update) | async-done | bytes 3276816 | tf_op jit(solution)/shard_map/all_gather | solution.py:207
  139.9 4.3 %fusion.8 = f32[256,1280]{1,0:T(8,128)} fusion(bf16[256,1280]{0,1:T(8,128)(2,1)} %bitcast.96, bf16[1280,1280]{1,0:T(8,128)(2,1)} %all-gather.7.cloned.1.call-done, bf16[1,256,1280]{2,1,0:T(8,128)(2,1)S(1)} %get-tuple-element.30, f32[1280]{0:T(1024)S(1)} %copy-done.9), kind=kOutput, calls=%fused_computation.24 | convolution fusion | flops 840499200 | bytes 5903360 | tf_op jit(solution)/shard_map/dot_general | solution.py:122
  144.1 1.7 reshape.608
  145.8 1.6 reduce_sum.78
  147.4 1.0 fusion.39
  148.4 1.7 gather_fusion.2
  150.1 0.1 bitcast_select_fusion
  150.2 0.5 broadcast.701
  150.7 0.8 reduce.6
  151.6 0.8 reshape.651
  152.4 7.4 %all-to-all-start = ((bf16[128,2,640]{2,1,0:T(2,128)(2,1)}), bf16[128,2,640]{2,1,0:T(2,128)(2,1)S(1)}, u32[]{:S(2)}, u32[]{:S(2)}) async-start(bf16[128,2,640]{2,1,0:T(2,128)(2,1)} %reshape.651), calls=%async_computation | async-start | bytes 655360 | tf_op jit(solution)/shard_map/all_to_all | solution.py:222
  159.8 0.2 all-gather.9.cloned.1.call-start
  160.1 11.6 %all-to-all-done = bf16[128,2,640]{2,1,0:T(2,128)(2,1)S(1)} async-done(((bf16[128,2,640]{2,1,0:T(2,128)(2,1)}), bf16[128,2,640]{2,1,0:T(2,128)(2,1)S(1)}, u32[]{:S(2)}, u32[]{:S(2)}) %all-to-all-start) | async-done | bytes 327712 | tf_op jit(solution)/shard_map/all_to_all | solution.py:222
  171.7 0.3 reshape.652
  172.0 0.9 gather_fusion.4
  172.9 6.3 %multiply_reduce_fusion = (f32[128]{0:T(128)S(1)}, f32[128,4096]{1,0:T(8,128)S(1)}) fusion(bf16[128,1,4096]{2,0,1:T(8,128)(2,1)} %param.22, f32[4096]{0:T(1024)S(1)} %copy-done.4, bf16[128,1280]{1,0:T(8,128)(2,1)S(1)} %gather_fusion.4, bf16[1280,4096]{1,0:T(8,128)(2,1)} %param.29, pred[128]{0:T(512)(128)(4,1)S(1)} %get-tuple-element.47), kind=kOutput, calls=%fused_computation.26 | convolution fusion | flops 1345322880 | bytes 13976192 | tf_op jit(solution)/shard_map/dot_general | solution.py:232
  179.2 1.3 multiply_convert_fusion
  180.5 0.0 all-gather.9.cloned.1.call-update
  180.5 0.0 all-gather.11.cloned.1.call-start
  180.6 46.0 %all-gather.9.cloned.1.call-done = bf16[1024,4096]{1,0:T(8,128)(2,1)} async-done(((bf16[128,4096]{1,0:T(8,128)(2,1)}), bf16[1024,4096]{1,0:T(8,128)(2,1)}) %all-gather.9.cloned.1.call-update) | async-done | bytes 8388624 | tf_op jit(solution)/shard_map/all_gather | solution.py:243
  226.6 6.4 %convolution_bitcast_fusion = f32[1024,1,128]{0,2,1:T(8,128)S(1)} fusion(bf16[1024,4096]{1,0:T(8,128)(2,1)} %all-gather.9.cloned.1.call-done, bf16[4096,128]{1,0:T(8,128)(2,1)S(1)} %copy-done.2), kind=kOutput, calls=%fused_computation.41 | convolution fusion | flops 1073741824 | bytes 9961472 | tf_op jit(solution)/shard_map/dot_general | solution.py:247
  233.0 1.2 fusion.41
  234.2 2.9 convolution_convert_fusion.1
  237.1 0.8 pad_maximum_fusion
  238.0 0.0 all-gather.11.cloned.1.call-update
  238.0 0.3 reduce-scatter.2.cloned.1.call-start
  238.3 3.1 multiply_cosine_fusion
  241.3 6.3 %fusion.69 = f32[1024,256]{0,1:T(8,128)S(1)} fusion(bf16[1024,4096]{1,0:T(8,128)(2,1)} %all-gather.9.cloned.1.call-done, bf16[4096,256]{1,0:T(8,128)(2,1)} %param.32), kind=kOutput, calls=%fused_computation.159 | convolution fusion | flops 2147483648 | bytes 11534336 | tf_op jit(solution)/shard_map/dot_general | solution.py:246
  247.7 1.1 fusion.67
  248.8 1.5 copy.52
  250.3 2.2 copy.51
  252.5 2.3 multiply_subtract_fusion
  254.8 1.3 fusion.21
  256.1 1.1 convert_element_type.106.q_ref
  257.2 51.5 %all-gather.11.cloned.1.call-done = bf16[16384,256]{0,1:T(8,128)(2,1)} async-done(((bf16[1024,256]{0,1:T(8,128)(2,1)}), bf16[16384,256]{0,1:T(8,128)(2,1)}) %all-gather.11.cloned.1.call-update) | async-done | bytes 8388624 | tf_op jit(solution)/shard_map/all_gather | solution.py:280
  308.8 11.9 %copy.48 = bf16[16384,256]{1,0:T(8,128)(2,1)} copy(bf16[16384,256]{0,1:T(8,128)(2,1)} %all-gather.11.cloned.1.call-done) | data formatting | bytes 16777216 | tf_op jit(solution)/shard_map/all_gather | solution.py:280
  320.7 38.3 %attend.1 = bf16[8,128,256]{2,1,0:T(8,128)(2,1)} custom-call(s32[1]{0:T(128)} %bitcast.seq_ref, bf16[8,128,256]{2,1,0:T(8,128)(2,1)} %convert_element_type.106.q_ref, bf16[128,128,256]{2,1,0:T(8,128)(2,1)} %bitcast.90), custom_call_target="tpu_custom_call" | custom-call | tf_op jit(solution)/shard_map/attend/pallas_call | solution.py:86
  359.0 6.6 %convolution_convert_fusion = bf16[1024,4096]{1,0:T(8,128)(2,1)} fusion(bf16[1024,256]{1,0:T(8,128)(2,1)} %bitcast.94, bf16[256,4096]{1,0:T(8,128)(2,1)S(1)} %copy-done), kind=kOutput, calls=%fused_computation.6 | convolution fusion | flops 2151677952 | bytes 11010048 | tf_op jit(solution)/shard_map/dot_general | solution.py:289
  365.6 0.0 reduce-scatter.2.cloned.1.call-update
  365.6 51.8 %reduce-scatter.2.cloned.1.call-done = bf16[128,4096]{1,0:T(8,128)(2,1)} async-done(((bf16[1024,4096]{1,0:T(8,128)(2,1)}), bf16[128,4096]{1,0:T(8,128)(2,1)}) %reduce-scatter.2.cloned.1.call-update) | async-done | bytes 1048592 | tf_op jit(solution)/shard_map/reduce_scatter | solution.py:288
  (36 shorter events, 0.2 us)
Async XLA Ops:
  6.5 352.4 %copy-start = (bf16[256,4096]{1,0:T(8,128)(2,1)S(1)}, bf16[256,4096]{1,0:T(8,128)(2,1)}, u32[]{:S(2)}) copy-start(bf16[256,4096]{1,0:T(8,128)(2,1)} %param.35) | copy-start | bytes 6291460
  6.5 83.5 %all-gather.5.cloned.1.call-start = ((), (), s32[]{:S(2)}) async-start(), calls=%async_computation.2 | async-start | bytes 10444800 | tf_op jit(solution)/shard_map/all_gather | solution.py:191
  7.3 132.6 %all-gather.7.cloned.1.call-start = ((), (), s32[]{:S(2)}) async-start(), calls=%async_computation.3 | async-start | bytes 3481600 | tf_op jit(solution)/shard_map/all_gather | solution.py:207
  8.0 19.4 %collective-permute-start = (bf16[2,256,1280]{2,1,0:T(8,128)(2,1)}, bf16[2,256,1280]{2,1,0:T(8,128)(2,1)}, u32[]{:S(2)}, u32[]{:S(2)}) collective-permute-start(bf16[2,256,1280]{2,1,0:T(8,128)(2,1)} %param.18), channel_id=1, source_target_pairs={{0,16},{16,0},{32,48},{48,32},{64,80},{80,64},{96,112},{112,96},{1... | collective-permute-start | bytes 3932168 | tf_op jit(solution)/shard_map/ppermute | solution.py:23
  24.6 65.4 %copy-start.6 = (f32[3840]{0:T(1024)S(1)}, f32[3840]{0:T(1024)}, u32[]{:S(2)}) copy-start(f32[3840]{0:T(1024)} %param.26) | copy-start | bytes 46084
  24.6 65.4 %copy-start.7 = (f32[1280]{0:T(1024)S(1)}, f32[1280]{0:T(1024)}, u32[]{:S(2)}) copy-start(f32[1280]{0:T(1024)} %param.24) | copy-start | bytes 15364
  24.6 65.4 %copy-start.8 = (f32[1280]{0:T(1024)S(1)}, f32[1280]{0:T(1024)}, u32[]{:S(2)}) copy-start(f32[1280]{0:T(1024)} %param.23) | copy-start | bytes 15364
  105.7 34.1 %copy-start.9 = (f32[1280]{0:T(1024)S(1)}, f32[1280]{0:T(1024)}, u32[]{:S(2)}) copy-start(f32[1280]{0:T(1024)} %param.28) | copy-start | bytes 15364
  152.4 19.3 %all-to-all-start = ((bf16[128,2,640]{2,1,0:T(2,128)(2,1)}), bf16[128,2,640]{2,1,0:T(2,128)(2,1)S(1)}, u32[]{:S(2)}, u32[]{:S(2)}) async-start(bf16[128,2,640]{2,1,0:T(2,128)(2,1)} %reshape.651), calls=%async_computation | async-start | bytes 655360 | tf_op jit(solution)/shard_map/all_to_all | solution.py:222
  159.8 66.8 %all-gather.9.cloned.1.call-start = ((), (), s32[]{:S(2)}) async-start(), calls=%async_computation.4 | async-start | bytes 9437184 | tf_op jit(solution)/shard_map/all_gather | solution.py:243
  172.0 1.0 copy-start.4
  172.9 6.3 %copy-start.5 = (f32[4096]{0:T(1024)S(1)}, f32[4096]{0:T(1024)}, u32[]{:S(2)}) copy-start(f32[4096]{0:T(1024)} %param.31) | copy-start | bytes 49156
  179.2 47.4 %copy-start.2 = (bf16[4096,128]{1,0:T(8,128)(2,1)S(1)}, bf16[4096,128]{1,0:T(8,128)(2,1)}, u32[]{:S(2)}) copy-start(bf16[4096,128]{1,0:T(8,128)(2,1)} %param.33) | copy-start | bytes 3145732
  180.5 128.2 %all-gather.11.cloned.1.call-start = ((), (), s32[]{:S(2)}) async-start(), calls=%async_computation.5 | async-start | bytes 8912896 | tf_op jit(solution)/shard_map/all_gather | solution.py:280
  226.6 7.6 %copy-start.1 = (bf16[1024,4096]{1,0:T(8,128)(2,1)S(1)}, bf16[1024,4096]{1,0:T(8,128)(2,1)}, u32[]{:S(2)}) copy-start(bf16[1024,4096]{1,0:T(8,128)(2,1)} %all-gather.9.cloned.1.call-done) | copy-start | bytes 25165828
  226.6 7.6 %copy-start.3 = (bf16[4096,128]{1,0:T(8,128)(2,1)S(1)}, bf16[4096,128]{1,0:T(8,128)(2,1)}, u32[]{:S(2)}) copy-start(bf16[4096,128]{1,0:T(8,128)(2,1)} %param.34) | copy-start | bytes 3145732
  238.0 179.4 %reduce-scatter.2.cloned.1.call-start = ((), (), s32[]{:S(2)}) async-start(), calls=%async_computation.6 | async-start | bytes 9437184 | tf_op jit(solution)/shard_map/reduce_scatter | solution.py:288
Sparse Core Ops, SparseCore 0:
  9.5 80.4 all-gather.4
  92.2 47.5 all-gather.6
  180.6 45.9 all-gather.8
  238.1 70.6 all-gather.10
  365.7 51.6 reduce-scatter.1
